TPU v7x, 32 devices: a whole 2x2x4 slice. The times are simulated.
32 devices in a mesh: dp: 4 (over y, x), rep: 8 (over z, core).
Axes of the slice: x: 2, y: 2, z: 4, core: 2. Of those that a mesh axis runs over, the one named last changes fastest.
Arguments:
- queries: bfloat16 [16384, 2048], P(('dp', 'rep')), may hold values from -32 to 32
- key_rows: bfloat16 [16384, 2048], P(('dp', 'rep')), may hold values from -32 to 32
- values: bfloat16 [16384, 2048], P(('dp', 'rep')), may hold values from -6 to 6
- upstream: bfloat16 [16384, 2048], P(('dp', 'rep')), may hold values from -6 to 6
- out_weight: bfloat16 [2048, 2048], P(('dp', 'rep')), may hold values from -0.125 to 0.125
- sample_ids: int32 [32, 512], P(('dp', 'rep')), may hold values from 0 to 3, as said below
Outputs:
- grad_queries: bfloat16 [16384, 2048], P(('dp', 'rep'))
- grad_keys: bfloat16 [16384, 2048], P(('dp', 'rep'))
- grad_values: bfloat16 [16384, 2048], P(('dp', 'rep'))
- grad_weight: float32 [2048, 2048], P(('dp', 'rep'))
Inputs may be any that keep to these rules, and one draw needn't show every extreme that they name: `sample_ids`: within a row the ids never fall, every row starts with 0 and ends with 3, and the tokens of one sample are contiguous.
All inputs are finite; a program needn't handle non-finite values.
Results may differ from a plain program's by a relative error of at most 0.015.
Values may be sent and summed in bfloat16 or wider, within the bound.
A program may use at most 192 MiB of HBM per device.

v0:
```python
import math

import jax
import jax.numpy as jnp
from jax import lax
from jax.sharding import PartitionSpec as P

H = 16
DH = 128


def allowed_pairs(ids_row):
    positions = jnp.arange(ids_row.shape[0], dtype=jnp.int32)
    causal = positions[None, :] <= positions[:, None]
    return jnp.logical_and(causal, ids_row[None, :] == ids_row[:, None])[None]


def attend_forward(query_block, key_block, value_block, ids_row):
    scaling = 1.0 / math.sqrt(DH)
    scores = (
        jnp.einsum("qhd,khd->hqk", query_block, key_block, preferred_element_type=jnp.float32)
        * scaling
    )
    allowed = allowed_pairs(ids_row)
    masked = jnp.where(allowed, scores, -jnp.inf)
    row_max = jnp.max(masked, axis=2, keepdims=True)
    raised = jnp.where(allowed, jnp.exp(masked - row_max), 0.0)
    probabilities = raised / jnp.sum(raised, axis=2, keepdims=True)
    probs_low = probabilities.astype(jnp.bfloat16)
    attended = jnp.einsum(
        "hqk,khd->qhd", probs_low, value_block, preferred_element_type=jnp.float32
    ).astype(jnp.bfloat16)
    return (probabilities, probs_low, attended)


def attend_backward(probabilities, probs_low, query_block, key_block, value_block, grad_block):
    scaling = 1.0 / math.sqrt(DH)
    grad_values = jnp.einsum(
        "hqk,qhd->khd", probs_low, grad_block, preferred_element_type=jnp.float32
    ).astype(jnp.bfloat16)
    grad_probs = jnp.einsum(
        "qhd,khd->hqk", grad_block, value_block, preferred_element_type=jnp.float32
    )
    row_inner = jnp.sum(probabilities * grad_probs, axis=2, keepdims=True)
    grad_scores = (probabilities * (grad_probs - row_inner)).astype(jnp.bfloat16)
    grad_queries = (
        scaling
        * jnp.einsum("hqk,khd->qhd", grad_scores, key_block, preferred_element_type=jnp.float32)
    ).astype(jnp.bfloat16)
    grad_keys = (
        scaling
        * jnp.einsum("hqk,qhd->khd", grad_scores, query_block, preferred_element_type=jnp.float32)
    ).astype(jnp.bfloat16)
    return (grad_queries, grad_keys, grad_values)


def shards(queries, key_rows, values, upstream, out_weight, sample_ids):
    seq_count = sample_ids.shape[0]
    seq_len = sample_ids.shape[1]
    tok_rows = queries.shape[0]
    hidden_width = queries.shape[1]
    total_tokens = tok_rows * lax.axis_size("dp") * lax.axis_size("rep")
    split_shape = (seq_count, seq_len, H, DH)
    query_seqs = queries.reshape(split_shape)
    key_seqs = key_rows.reshape(split_shape)
    value_seqs = values.reshape(split_shape)
    seq_index = 0
    probabilities, probs_low, attended = attend_forward(
        query_seqs[seq_index], key_seqs[seq_index], value_seqs[seq_index], sample_ids[seq_index]
    )
    kept_probs = [(probabilities, probs_low)]
    attended_parts = attended.reshape(seq_len, hidden_width)
    columns = upstream
    group_sums = lax.psum_scatter(
        lax.dot_general(
            columns, attended_parts, (((0,), (0,)), ((), ())), preferred_element_type=jnp.float32
        ).astype(jnp.bfloat16),
        "dp",
        scatter_dimension=0,
        tiled=True,
    )
    summed = lax.psum_scatter(group_sums, "rep", scatter_dimension=0, tiled=True).astype(
        jnp.float32
    )
    grad_weight = summed * (1.0 / math.sqrt(total_tokens))
    columns = upstream
    attended_sums = jnp.dot(
        columns,
        lax.all_gather(out_weight, ("dp", "rep"), axis=0, tiled=True),
        preferred_element_type=jnp.float32,
    )
    grad_attended = attended_sums.astype(jnp.bfloat16).reshape(split_shape)
    seq_index = 0
    probabilities, probs_low = kept_probs[seq_index]
    grad_queries, grad_keys, grad_values = attend_backward(
        probabilities,
        probs_low,
        query_seqs[seq_index],
        key_seqs[seq_index],
        value_seqs[seq_index],
        grad_attended[seq_index],
    )
    query_parts = grad_queries.reshape(seq_len, hidden_width)
    key_parts = grad_keys.reshape(seq_len, hidden_width)
    value_parts = grad_values.reshape(seq_len, hidden_width)
    return (query_parts, key_parts, value_parts, grad_weight)


def solution(mesh):
    in_specs = (
        P(("dp", "rep"), None),
        P(("dp", "rep"), None),
        P(("dp", "rep"), None),
        P(("dp", "rep"), None),
        P(("dp", "rep"), None),
        P(("dp", "rep"), None),
    )
    out_specs = (
        P(("dp", "rep"), None),
        P(("dp", "rep"), None),
        P(("dp", "rep"), None),
        P(("dp", "rep"), None),
    )
    return jax.shard_map(shards, mesh=mesh, in_specs=in_specs, out_specs=out_specs, check_vma=False)
```

profile of v0, /device:TPU:0, one launch (start us, length us, event | category | flops | bytes accessed | tf_op | source)
XLA Modules:
  0.0 203.2 jit_solution(8849140755359418351)
XLA Ops:
  8.0 0.0 copy-start
  8.0 0.0 all-gather.2.cloned.1.call-start
  8.1 0.7 all-gather.2.cloned.1.call-update
  8.7 0.0 reduce-scatter.5.cloned.1.call-start
  8.8 4.0 %copy.49 = bf16[512,2048]{0,1:T(8,128)(2,1)} copy(bf16[512,2048]{1,0:T(8,128)(2,1)} %param.6) | data formatting | bytes 4194304 | tf_op jit(solution)/shard_map/squeeze;reshape | solution.py:69
  12.8 0.0 copy-start.6
  12.8 3.9 %copy.48 = bf16[512,2048]{0,1:T(8,128)(2,1)} copy(bf16[512,2048]{1,0:T(8,128)(2,1)} %param.7) | data formatting | bytes 4194304 | tf_op jit(solution)/shard_map/squeeze;reshape | solution.py:99
  16.7 3.9 %copy.51 = bf16[512,2048]{0,1:T(8,128)(2,1)} copy(bf16[512,2048]{1,0:T(8,128)(2,1)} %param.8) | data formatting | bytes 4194304 | tf_op jit(solution)/shard_map/squeeze;reshape | solution.py:100
  20.6 0.0 copy-done.6
  20.6 0.2 fusion.17
  20.8 12.0 %fusion.20 = (f32[16,512]{1,0:T(8,128)S(1)}, f32[16,512,512]{1,2,0:T(8,128)}) fusion(pred[512,512]{0,1:T(8,128)(4,1)S(1)} %fusion.17, bf16[512,16,128]{0,2,1:T(8,128)(2,1)} %bitcast.39, bf16[512,16,128]{0,2,1:T(8,128)(2,1)} %bitcast.36), kind=kOutput, calls=%fused_computation.26 | convolution fusion | flops 1094713856 | bytes 21266432 | tf_op jit(solution)/shard_map/sub | solution.py:27
  32.8 7.7 %fusion.12 = bf16[16,512,128]{1,2,0:T(8,128)(2,1)S(1)} fusion(bf16[512,16,128]{0,2,1:T(8,128)(2,1)} %bitcast.41, f32[16,512,512]{1,2,0:T(8,128)} %get-tuple-element.13, f32[16,512]{1,0:T(8,128)S(1)} %get-tuple-element.12), kind=kOutput, calls=%fused_computation.19 | convolution fusion | flops 1083179008 | bytes 21004288 | tf_op jit(solution)/shard_map/hqk,khd->qhd/dot_general | solution.py:30
  40.5 0.0 copy-done
  40.5 6.8 %convert_bitcast_fusion = bf16[2048,2048]{0,1:T(8,128)(2,1)} fusion(bf16[512,2048]{0,1:T(8,128)(2,1)S(1)} %bitcast.48, bf16[512,2048]{1,0:T(8,128)(2,1)S(1)} %copy-done), kind=kOutput, calls=%fused_computation.6 | convolution fusion | flops 4299161600 | bytes 12582912 | tf_op jit(solution)/shard_map/dot_general | solution.py:75
  47.3 0.0 reduce-scatter.5.cloned.1.call-update
  47.3 0.2 reduce-scatter.7.cloned.1.call-start
  47.6 50.7 %all-gather.2.cloned.1.call-done = bf16[2048,2048]{1,0:T(8,128)(2,1)} async-done(((bf16[64,2048]{1,0:T(8,128)(2,1)}), bf16[2048,2048]{1,0:T(8,128)(2,1)}) %all-gather.2.cloned.1.call-update) | async-done | bytes 8388624 | tf_op jit(solution)/shard_map/all_gather | solution.py:89
  98.3 9.3 %convolution_convert_fusion = bf16[512,2048]{1,0:T(8,128)(2,1)} fusion(bf16[512,2048]{1,0:T(8,128)(2,1)S(1)} %copy-done, bf16[2048,2048]{1,0:T(8,128)(2,1)} %all-gather.2.cloned.1.call-done), kind=kOutput, calls=%fused_computation.17 | convolution fusion | flops 4296015872 | bytes 12582912 | tf_op jit(solution)/shard_map/dot_general | solution.py:87
  107.6 2.9 %copy.50 = bf16[512,2048]{0,1:T(8,128)(2,1)S(1)} copy(bf16[512,2048]{1,0:T(8,128)(2,1)} %convolution_convert_fusion) | data formatting | bytes 4194304 | tf_op jit(solution)/shard_map/squeeze;reshape | solution.py:101
  110.5 0.0 copy-start.5
  110.5 1.3 copy-done.5
  111.8 10.0 %fusion.9 = bf16[16,128,512]{2,1,0:T(8,128)(2,1)} fusion(bf16[512,16,128]{0,2,1:T(8,128)(2,1)S(1)} %bitcast.43, f32[16,512,512]{1,2,0:T(8,128)} %get-tuple-element.13, f32[16,512]{1,0:T(8,128)S(1)} %get-tuple-element.12), kind=kOutput, calls=%fused_computation.18 | convolution fusion | flops 1083179008 | bytes 21004288 | tf_op jit(solution)/shard_map/hqk,qhd->khd/dot_general | solution.py:38
  121.8 0.0 copy-start.4
  121.8 4.1 %copy.40 = bf16[512,2048]{1,0:T(8,128)(2,1)} copy(bf16[512,2048]{0,1:T(8,128)(2,1)} %bitcast.46) | data formatting | bytes 4194304
  125.9 0.0 copy-done.4
  125.9 11.4 %multiply_reduce_fusion = (f32[16,512]{1,0:T(8,128)S(1)}, f32[16,512,512]{1,2,0:T(8,128)}) fusion(f32[16,512,512]{1,2,0:T(8,128)} %get-tuple-element.13, f32[16,512]{1,0:T(8,128)S(1)} %get-tuple-element.12, bf16[512,16,128]{0,2,1:T(8,128)(2,1)} %bitcast.44, bf16[512,16,128]{0,2,1:T(8,128)(2,1)S(1)} %bitcast.42), kind=kOutput, calls=%fused_computation.2 | convolution fusion | flops 1086316544 | bytes 37814272 | tf_op jit(solution)/shard_map/qhd,khd->hqk/dot_general | solution.py:41
  137.3 14.1 %reduce-scatter.5.cloned.1.call-done = bf16[512,2048]{0,1:T(8,128)(2,1)} async-done(((bf16[2048,2048]{0,1:T(8,128)(2,1)}), bf16[512,2048]{0,1:T(8,128)(2,1)}) %reduce-scatter.5.cloned.1.call-update) | async-done | bytes 2097168 | tf_op jit(solution)/shard_map/reduce_scatter | solution.py:74
  151.3 3.9 %copy.46 = bf16[512,2048]{1,0:T(8,128)(2,1)} copy(bf16[512,2048]{0,1:T(8,128)(2,1)} %reduce-scatter.5.cloned.1.call-done) | data formatting | bytes 4194304
  155.3 0.0 reduce-scatter.7.cloned.1.call-update
  155.3 0.0 copy-start.3
  155.3 11.9 %multiply_convert_fusion = bf16[16,512,512]{1,2,0:T(8,128)(2,1)S(1)} fusion(f32[16,512,512]{1,2,0:T(8,128)} %get-tuple-element.15, f32[16,512]{1,0:T(8,128)S(1)} %get-tuple-element.14, f32[16,512,512]{1,2,0:T(8,128)} %get-tuple-element.13, f32[16,512]{1,0:T(8,128)S(1)} %get-tuple-element.12), kind=kLoop, calls=%fused_computation.1 | loop fusion | flops 16777216 | bytes 42008576 | tf_op jit(solution)/shard_map/convert_element_type | solution.py:45
  167.2 0.0 copy-done.3
  167.2 0.0 copy-start.2
  167.2 3.2 %multiply_convert_fusion.2 = bf16[16,512,128]{1,2,0:T(8,128)(2,1)} fusion(bf16[512,16,128]{0,2,1:T(8,128)(2,1)S(1)} %bitcast.37, bf16[16,512,512]{1,2,0:T(8,128)(2,1)S(1)} %multiply_convert_fusion), kind=kOutput, calls=%fused_computation.16 | convolution fusion | flops 1075838976 | bytes 12582912 | tf_op jit(solution)/shard_map/hqk,khd->qhd/dot_general | solution.py:48
  170.4 0.8 copy-done.2
  171.2 3.9 %copy.38 = bf16[512,2048]{1,0:T(8,128)(2,1)} copy(bf16[512,2048]{0,1:T(8,128)(2,1)} %bitcast.38) | data formatting | bytes 4194304
  175.1 0.0 copy-start.1
  175.1 8.4 %multiply_convert_fusion.1 = bf16[16,512,128]{1,2,0:T(8,128)(2,1)} fusion(bf16[16,512,512]{1,2,0:T(8,128)(2,1)} %copy-done.2, bf16[512,16,128]{0,2,1:T(8,128)(2,1)} %bitcast.40), kind=kOutput, calls=%fused_computation.15 | convolution fusion | flops 1075838976 | bytes 12582912 | tf_op jit(solution)/shard_map/hqk,qhd->khd/dot_general | solution.py:52
  183.6 3.9 %copy.39 = bf16[512,2048]{1,0:T(8,128)(2,1)} copy(bf16[512,2048]{0,1:T(8,128)(2,1)} %bitcast.45) | data formatting | bytes 4194304
  187.5 4.1 %reduce-scatter.7.cloned.1.call-done = bf16[64,2048]{1,0:T(8,128)(2,1)} async-done(((bf16[512,2048]{1,0:T(8,128)(2,1)}), bf16[64,2048]{1,0:T(8,128)(2,1)}) %reduce-scatter.7.cloned.1.call-update) | async-done | bytes 262160
  191.6 2.0 copy.47
  193.6 1.1 convert_multiply_fusion
  194.7 1.1 copy.41
  195.8 0.0 copy-done.1
Async XLA Ops:
  8.0 32.5 %copy-start = (bf16[512,2048]{1,0:T(8,128)(2,1)S(1)}, bf16[512,2048]{1,0:T(8,128)(2,1)}, u32[]{:S(2)}) copy-start(bf16[512,2048]{1,0:T(8,128)(2,1)} %param.9) | copy-start | bytes 6291460
  8.0 90.3 %all-gather.2.cloned.1.call-start = ((), (), s32[]{:S(2)}) async-start(), calls=%async_computation.2 | async-start | bytes 8650752 | tf_op jit(solution)/shard_map/all_gather | solution.py:89
  8.7 142.6 %reduce-scatter.5.cloned.1.call-start = ((), (), s32[]{:S(2)}) async-start(), calls=%async_computation.3 | async-start | bytes 10485760 | tf_op jit(solution)/shard_map/reduce_scatter | solution.py:74
  12.8 7.8 %copy-start.6 = (s32[1,512]{1,0:T(1,128)S(1)}, s32[1,512]{1,0:T(1,128)}, u32[]{:S(2)}) copy-start(s32[1,512]{1,0:T(1,128)} %param.11) | copy-start | bytes 6148
  47.3 144.3 %reduce-scatter.7.cloned.1.call-start = ((), (), s32[]{:S(2)}) async-start(), calls=%async_computation.4 | async-start | bytes 2359296
  110.5 1.3 copy-start.5
  121.8 4.1 %copy-start.4 = (bf16[512,2048]{0,1:T(8,128)(2,1)S(1)}, bf16[512,2048]{0,1:T(8,128)(2,1)}, u32[]{:S(2)}) copy-start(bf16[512,2048]{0,1:T(8,128)(2,1)} %copy.51) | copy-start | bytes 6291460
  155.3 11.9 %copy-start.3 = (bf16[512,2048]{0,1:T(8,128)(2,1)S(1)}, bf16[512,2048]{0,1:T(8,128)(2,1)}, u32[]{:S(2)}) copy-start(bf16[512,2048]{0,1:T(8,128)(2,1)} %copy.48) | copy-start | bytes 6291460
  167.2 4.0 %copy-start.2 = (bf16[16,512,512]{1,2,0:T(8,128)(2,1)}, bf16[16,512,512]{1,2,0:T(8,128)(2,1)S(1)}, u32[]{:S(2)}) copy-start(bf16[16,512,512]{1,2,0:T(8,128)(2,1)S(1)} %multiply_convert_fusion) | copy-start | bytes 25165828
  175.1 20.7 %copy-start.1 = (bf16[512,2048]{1,0:T(8,128)(2,1)S(1)}, bf16[512,2048]{1,0:T(8,128)(2,1)}, u32[]{:S(2)}) copy-start(bf16[512,2048]{1,0:T(8,128)(2,1)} %param.9) | copy-start | bytes 6291460
Sparse Core Ops, SparseCore 0:
  11.8 86.4 all-gather.1
Sparse Core Ops, SparseCore 1:
  47.4 103.9 reduce-scatter.4
  155.4 36.2 reduce-scatter.6
where the time goes:
time: 204 us; the launch traced here: 203 us
  waiting for transfers between devices  69.6 us (34%)
  matrix products  68.8 us (34%)
  local copies, waits for them, and re-layouts  35.7 us (18%)
  between operations  15.6 us (8%)
  other arithmetic  13.2 us (6%)
    all_gather x1, waiting for transfers between devices, shards(): lax.all_gather(out_weight, ('dp', 'rep'), axis=0, tiled=True)  50.7 us
    unnamed x20, local copies, waits for them, and re-layouts  21.1 us
    reduce_scatter x1, waiting for transfers between devices, shards(): lax.psum_scatter(lax.dot_general(columns, attended_parts, (((0,), (0,)),...  14.1 us
    sub x1, matrix products, attend_forward(): raised = jnp.where(allowed, jnp.exp(masked - row_max), 0.0)  12 us
    convert_element_type x1, other arithmetic, attend_backward(): (probabilities * (grad_probs - row_inner)).astype(jnp.bfloat16)  11.9 us
    dot_general x1, matrix products, attend_backward(): jnp.einsum('qhd,khd->hqk', grad_block, value_block, preferred_element_typ...  11.4 us
    dot_general x1, matrix products, attend_backward(): jnp.einsum('hqk,qhd->khd', probs_low, grad_block, preferred_element_type=...  10 us
    dot_general x1, matrix products, shards(): jnp.dot(columns, lax.all_gather(out_weight, ('dp', 'rep'), axis=0, tiled=...  9.3 us
  transfers between devices with their start and end apart: 3, of which 3 were waited for; matrix products, arithmetic and copies ran while one was open for 53% of the time, Pallas kernels for 0%

commit v1 on v0

v1 whole, which is shorter than its diff:
```python
import functools
import math

import jax
import jax.numpy as jnp
from jax import lax
from jax.experimental import pallas as pl
from jax.experimental.pallas import tpu as pltpu
from jax.sharding import PartitionSpec as P

DH = 128
MESH = pl.DeviceIdType.MESH
F32 = jnp.float32
BF16 = jnp.bfloat16
SCALING = 1.0 / math.sqrt(DH)
VMEM_LIMIT = 60 * 1024 * 1024


def dot_nt(a, b):
    return lax.dot_general(a, b, (((1,), (1,)), ((), ())), preferred_element_type=F32)


def dot_tn(a, b):
    return lax.dot_general(a, b, (((0,), (0,)), ((), ())), preferred_element_type=F32)


def dot_nn(a, b):
    return jnp.dot(a, b, preferred_element_type=F32)


def fill_bias(bias, ids_row, ids_col):
    size = bias.shape[0]
    rows = lax.broadcasted_iota(jnp.int32, (size, size), 0)
    cols = lax.broadcasted_iota(jnp.int32, (size, size), 1)
    allowed = jnp.logical_and(cols <= rows, ids_row[...] == ids_col[...])
    bias[...] = jnp.where(allowed, 0.0, -1e30).astype(F32)


def block_probs(q, k, bias):
    s = dot_nt(q, k) + bias
    e = jnp.exp((s - jnp.max(s, axis=1, keepdims=True)) * SCALING)
    return e * (1.0 / jnp.sum(e, axis=1, keepdims=True))


def head_forward(q_ref, k_ref, v_ref, o_ref, bias, cols):
    size = bias.shape[0]
    half = size // 2
    for at in range(2):
        rows, end = pl.ds(at * half, half), pl.ds(0, (at + 1) * half)
        p = block_probs(q_ref[rows, cols], k_ref[end, cols], bias[rows, end]).astype(BF16)
        o_ref[rows, cols] = dot_nn(p, v_ref[end, cols]).astype(BF16)


def head_backward(q_ref, k_ref, v_ref, g_ref, dq_ref, dk_ref, dv_ref, bias, cols):
    size = bias.shape[0]
    half = size // 2
    grads = []
    for at in range(2):
        rows, end = pl.ds(at * half, half), pl.ds(0, (at + 1) * half)
        q, k, v, g = q_ref[rows, cols], k_ref[end, cols], v_ref[end, cols], g_ref[rows, cols]
        p = block_probs(q, k, bias[rows, end])
        dv = dot_tn(p.astype(BF16), g)
        dp = dot_nt(g, v)
        inner = jnp.sum(p * dp, axis=1, keepdims=True)
        ds = (p * (dp - inner)).astype(BF16)
        dq_ref[rows, cols] = (dot_nn(ds, k) * SCALING).astype(BF16)
        grads.append((dot_tn(ds, q), dv))
    (dk0, dv0), (dk1, dv1) = grads
    top, low = pl.ds(0, half), pl.ds(half, half)
    dk_ref[top, cols] = ((dk0 + dk1[:half]) * SCALING).astype(BF16)
    dk_ref[low, cols] = (dk1[half:] * SCALING).astype(BF16)
    dv_ref[top, cols] = (dv0 + dv1[:half]).astype(BF16)
    dv_ref[low, cols] = dv1[half:].astype(BF16)


def forward_kernel(row_ref, col_ref, q_ref, k_ref, v_ref, o_ref, bias):
    @pl.when(pl.program_id(0) == 0)
    def _():
        fill_bias(bias, row_ref, col_ref)

    head_forward(q_ref, k_ref, v_ref, o_ref, bias, pl.ds(0, DH))


def backward_kernel(row_ref, col_ref, q_ref, k_ref, v_ref, g_ref, dq_ref, dk_ref, dv_ref, bias):
    @pl.when(pl.program_id(0) == 0)
    def _():
        fill_bias(bias, row_ref, col_ref)

    head_backward(
        q_ref, k_ref, v_ref, g_ref, dq_ref, dk_ref, dv_ref, bias, pl.ds(0, DH)
    )


def attention_call(kernel, ids, arrays, outs, flops):
    size = ids.shape[1]
    heads = arrays[0].shape[1] // DH
    block = pl.BlockSpec((size, DH), lambda h: (0, h))
    whole = [
        pl.BlockSpec((1, size), lambda h: (0, 0)),
        pl.BlockSpec((size, 1), lambda h: (0, 0)),
    ]
    result = pl.pallas_call(
        kernel,
        grid=(heads,),
        out_shape=[jax.ShapeDtypeStruct(arrays[0].shape, BF16)] * outs,
        in_specs=whole + [block] * len(arrays),
        out_specs=[block] * outs,
        scratch_shapes=[pltpu.VMEM((size, size), F32)],
        compiler_params=pltpu.CompilerParams(dimension_semantics=("arbitrary",)),
        cost_estimate=pl.CostEstimate(
            flops=flops * 2 * size * size * DH * heads,
            bytes_accessed=2 * size * DH * heads * (len(arrays) + outs),
            transcendentals=size * size * heads,
        ),
    )(ids, ids.reshape(size, 1), *arrays)
    return result


class Place:
    def __init__(self, n_rep):
        self.n_rep = n_rep
        self.line = n_rep // 2
        self.dp = lax.axis_index("dp")
        rep = lax.axis_index("rep")
        self.r = rep // 2
        self.c = rep % 2

    def across(self, bit):
        return self.dp + bit - 2 * bit * ((self.dp // bit) % 2)

    def shard(self, dp, r, c):
        return dp * self.n_rep + r * 2 + c

    def dev(self, dp, r, c):
        return (dp, r * 2 + c)

    def greet(self):
        barrier = pltpu.get_barrier_semaphore()

        def signal(dev):
            pl.semaphore_signal(barrier, inc=1, device_id=dev, device_id_type=MESH)

        for bit in (1, 2):
            signal(self.dev(self.across(bit), self.r, self.c))
        signal(self.dev(self.dp, self.r, 1 - self.c))

        @pl.when(self.r > 0)
        def _():
            signal(self.dev(self.dp, self.r - 1, self.c))

        @pl.when(self.r < self.line - 1)
        def _():
            signal(self.dev(self.dp, self.r + 1, self.c))

        inner = jnp.logical_and(self.r > 0, self.r < self.line - 1)

        @pl.when(inner)
        def _():
            pl.semaphore_wait(barrier, 5)

        @pl.when(jnp.logical_not(inner))
        def _():
            pl.semaphore_wait(barrier, 4 if self.line > 1 else 3)


def rcopy(src, dst, send, recv, dev):
    return pltpu.make_async_remote_copy(
        src_ref=src, dst_ref=dst, send_sem=send, recv_sem=recv, device_id=dev, device_id_type=MESH
    )


def gather_events(n_rep, w_ref, all_ref, zs, zr, ps, pr, cs, cr, own_sem):
    me = Place(n_rep)
    depth = w_ref.shape[0]
    half = depth // 2
    line = me.line
    order = ((1, 2), (2, 1))

    def rows(dp, r, c, piece=None):
        start = pl.multiple_of(me.shard(dp, r, c) * depth, depth)
        if piece is None:
            return all_ref.at[pl.ds(start, depth)]
        return all_ref.at[pl.ds(pl.multiple_of(start + piece * half, half), half)]

    def zcopy(s, up):
        to = me.r + (1 if up else -1)
        ref = rows(me.dp, s, me.c)
        return rcopy(ref, ref, zs.at[1 if up else 0, s], zr.at[s], me.dev(me.dp, to, me.c))

    def zrecv(s):
        ref = rows(me.dp, s, me.c)
        rcopy(ref, ref, zs.at[0, s], zr.at[s], me.dev(me.dp, me.r, 1 - me.c)).wait_recv()

    def pcopy(dp, s, piece, step):
        bit = order[piece][step]
        ref = rows(dp, s, me.c, piece)
        return rcopy(
            ref, ref, ps.at[dp, s, 2 * piece + step], pr.at[dp, s, piece],
            me.dev(me.across(bit), me.r, me.c),
        )

    def ccopy(dp, s, piece):
        ref = rows(dp, s, me.c, piece)
        return rcopy(
            ref, ref, cs.at[dp, s, piece], cr.at[dp, s, piece], me.dev(me.dp, me.r, 1 - me.c)
        )

    def crecv(dp, s, piece):
        ref = rows(dp, s, 1 - me.c, piece)
        rcopy(
            ref, ref, cs.at[dp, s, piece], cr.at[dp, s, piece], me.dev(me.dp, me.r, 1 - me.c)
        ).wait_recv()

    def first():
        own = pltpu.make_async_copy(w_ref, rows(me.dp, me.r, me.c), own_sem)
        own.start()
        me.greet()
        own.wait()

        @pl.when(me.r < line - 1)
        def _():
            zcopy(me.r, True).start()

        @pl.when(me.r > 0)
        def _():
            zcopy(me.r, False).start()

        spread(me.r)

    def spread(s):
        for piece in range(2):
            pcopy(me.dp, s, piece, 0).start()
        for piece in range(2):
            pcopy(me.dp, s, piece, 1).start()
        for piece in range(2):
            ccopy(me.dp, s, piece).start()

    def relay(s):
        for piece in range(2):
            src = me.across(order[piece][0])
            pcopy(src, s, piece, 0).wait_recv()
            pcopy(src, s, piece, 1).start()
            ccopy(src, s, piece).start()

    def last(s):
        for piece in range(2):
            near = me.across(order[piece][1])
            for dp in (near, 3 - me.dp):
                pcopy(dp, s, piece, 0).wait_recv()
                ccopy(dp, s, piece).start()

    def drain(s):
        for piece in range(2):
            near0 = me.across(order[piece][0])
            pcopy(me.dp, s, piece, 0).wait_send()
            pcopy(me.dp, s, piece, 1).wait_send()
            pcopy(near0, s, piece, 1).wait_send()
            for dp in (me.dp, me.across(1), me.across(2), 3 - me.dp):
                ccopy(dp, s, piece).wait_send()
                crecv(dp, s, piece)

    def each(d, act):
        if d == 0:
            act(me.r, 0)
            return

        @pl.when(me.r >= d)
        def _():
            act(me.r - d, 1)

        @pl.when(me.r + d < line)
        def _():
            act(me.r + d, -1)

    def arrive(s, side):
        zrecv(s)
        if side == 1:

            @pl.when(me.r < line - 1)
            def _():
                zcopy(s, True).start()

        else:

            @pl.when(me.r > 0)
            def _():
                zcopy(s, False).start()

        spread(s)

    def zdrain(s, side):
        if side >= 0:

            @pl.when(me.r < line - 1)
            def _():
                zcopy(s, True).wait_send()

        if side <= 0:

            @pl.when(me.r > 0)
            def _():
                zcopy(s, False).wait_send()

    events = [first]
    for d in range(line):
        events.append(lambda d=d: each(d, lambda s, side: relay(s)))
        if d + 1 < line:
            events.append(lambda d=d: each(d + 1, arrive))
        events.append(lambda d=d: each(d, lambda s, side: last(s)))

    def finish():
        for d in range(line):
            each(d, lambda s, side: drain(s))
            each(d, zdrain)

    events.append(finish)
    return events


def gather_scratch(n_dp, n_rep):
    line = n_rep // 2
    dma = pltpu.SemaphoreType.DMA
    return [
        dma((2, line)), dma((line,)),
        dma((n_dp, line, 4)), dma((n_dp, line, 2)),
        dma((n_dp, line, 2)), dma((n_dp, line, 2)),
        dma,
    ]


def gather_kernel(n_rep, w_ref, all_ref, *sems):
    for event in gather_events(n_rep, w_ref, all_ref, *sems):
        event()


def gather_weight(w, n_dp, n_rep):
    vm = pl.BlockSpec(memory_space=pltpu.VMEM)
    return pl.pallas_call(
        functools.partial(gather_kernel, n_rep),
        out_shape=jax.ShapeDtypeStruct((n_dp * n_rep * w.shape[0], w.shape[1]), w.dtype),
        in_specs=[vm],
        out_specs=vm,
        scratch_shapes=gather_scratch(n_dp, n_rep),
        compiler_params=pltpu.CompilerParams(
            collective_id=0, has_side_effects=True, vmem_limit_bytes=VMEM_LIMIT
        ),
    )(w)


def shards(queries, key_rows, values, upstream, out_weight, sample_ids):
    n_dp, n_rep = lax.axis_size("dp"), lax.axis_size("rep")
    total_tokens = queries.shape[0] * n_dp * n_rep
    square = n_dp == 4 and n_rep % 2 == 0
    qkv = (queries, key_rows, values)
    (attended,) = attention_call(forward_kernel, sample_ids, qkv, 1, 2)
    part = lax.dot_general(
        upstream, attended, (((0,), (0,)), ((), ())), preferred_element_type=F32
    ).astype(BF16)
    group_sums = lax.psum_scatter(part, "dp", scatter_dimension=0, tiled=True)
    summed = lax.psum_scatter(group_sums, "rep", scatter_dimension=0, tiled=True)
    grad_weight = summed.astype(F32) * (1.0 / math.sqrt(total_tokens))
    if square:
        weight = gather_weight(out_weight, n_dp, n_rep)
    else:
        weight = lax.all_gather(out_weight, ("dp", "rep"), axis=0, tiled=True)
    grad_attended = jnp.dot(upstream, weight, preferred_element_type=F32).astype(BF16)
    grads = attention_call(backward_kernel, sample_ids, qkv + (grad_attended,), 3, 5)
    return (*grads, grad_weight)


def solution(mesh):
    spec = P(("dp", "rep"), None)
    return jax.shard_map(
        shards, mesh=mesh, in_specs=(spec,) * 6, out_specs=(spec,) * 4, check_vma=False
    )
```

time: 204 us -> 229 us (1.12)
  Pallas kernels: 0 us -> 97.6 us
  matrix products: 68.8 us -> 17.4 us
  local copies, waits for them, and re-layouts: 35.7 us -> 8.71 us
  waiting for transfers between devices: 69.6 us -> 89.1 us
  other arithmetic: 13.2 us -> 1.11 us
    pallas_call x0 -> x3, Pallas kernels: none -> 97.6 us  [the longest x1 53.8 us: gather_weight(): pl.pallas_call(functools.partial(gather_kernel, n_rep), out_shape=jax.Sha...]
    reduce_scatter x1, waiting for transfers between devices: 14.1 us -> 89.1 us  [shards(): group_sums = lax.psum_scatter(part, 'dp', scatter_dimension=0, tiled=True)]
    all_gather x1 -> x0, waiting for transfers between devices: 50.7 us -> none  [shards(): lax.all_gather(out_weight, ('dp', 'rep'), axis=0, tiled=True)]
    dot_general x7 -> x2, matrix products: 56.7 us -> 17.4 us  [the longest x1 9.05 us: shards(): jnp.dot(upstream, weight, preferred_element_type=F32).astype(BF16)]
    another operation x4 -> x0, local copies, waits for them, and re-layouts: 14.7 us -> none  [the longest x1 3.95 us: shards(): query_seqs[seq_index]]
    unnamed x20 -> x5, local copies, waits for them, and re-layouts: 21.1 us -> 7.03 us
    sub x1 -> x0, matrix products: 12 us -> none  [attend_forward(): raised = jnp.where(allowed, jnp.exp(masked - row_max), 0.0)]
    convert_element_type x1 -> x0, other arithmetic: 11.9 us -> none  [attend_backward(): (probabilities * (grad_probs - row_inner)).astype(jnp.bfloat16)]
  transfers between devices with their start and end apart: 3 -> 2, of which waited for: 3 -> 1; matrix products, arithmetic and copies ran while one was open for 53% -> 4% of each run, Pallas kernels for 0% -> 35%
where the time goes in v1:
time: 229 us; the launch traced here: 228 us
  Pallas kernels  97.6 us (43%)
  waiting for transfers between devices  89.1 us (39%)
  matrix products  17.4 us (8%)
  between operations  14.1 us (6%)
  local copies, waits for them, and re-layouts  8.71 us (4%)
    reduce_scatter x1, waiting for transfers between devices, shards(): group_sums = lax.psum_scatter(part, 'dp', scatter_dimension=0, tiled=True)  89.1 us
    pallas_call x1, Pallas kernels, gather_weight(): pl.pallas_call(functools.partial(gather_kernel, n_rep), out_shape=jax.Sha...  53.8 us
    pallas_call x2, Pallas kernels, attention_call(): pl.pallas_call(kernel, grid=(heads,), out_shape=[jax.ShapeDtypeStruct(arr...  43.8 us
    dot_general x1, matrix products, shards(): jnp.dot(upstream, weight, preferred_element_type=F32).astype(BF16)  9.05 us
    dot_general x1, matrix products, shards(): lax.dot_general(upstream, attended, (((0,), (0,)), ((), ())), preferred_e...  8.38 us
    unnamed x5, local copies, waits for them, and re-layouts  7.03 us
  transfers between devices with their start and end apart: 2, of which 1 were waited for; matrix products, arithmetic and copies ran while one was open for 4% of the time, Pallas kernels for 35%

profile of v1, /device:TPU:0, one launch (start us, length us, event | category | flops | bytes accessed | tf_op | source)
XLA Modules:
  0.0 228.2 jit_solution(10818236826932242492)
XLA Ops:
  7.2 0.0 copy-start
  7.2 0.0 reduce-scatter.5.cloned.1.call-start
  7.2 1.7 copy.14.col_ref
  8.9 18.6 %shard_map.95 = bf16[512,2048]{1,0:T(8,128)(2,1)} custom-call(s32[1,512]{1,0:T(1,128)} %row_ref.3, s32[512,1]{1,0:T(8,128)} %copy.14.col_ref, bf16[512,2048]{1,0:T(8,128)(2,1)} %q_ref.3, bf16[512,2048]{1,0:T(8,128)(2,1)} %k_ref.3, bf16[512,2048]{1,0:T(8,128)(2,1)} %v_ref.3), custom_call_target="tpu_custom_call" | custom-call | flops 2147483648 | bytes 8388608 | tf_op jit(solution)/shard_map/pallas_call | solution.py:102
  27.5 0.0 copy-done
  27.5 8.4 %convert_bitcast_fusion = bf16[2048,2048]{0,1:T(8,128)(2,1)} fusion(bf16[512,2048]{1,0:T(8,128)(2,1)} %shard_map.95, bf16[512,2048]{1,0:T(8,128)(2,1)S(1)} %copy-done), kind=kOutput, calls=%fused_computation | convolution fusion | flops 4299161600 | bytes 12582912 | tf_op jit(solution)/shard_map/dot_general | solution.py:356
  35.9 0.0 reduce-scatter.5.cloned.1.call-update
  36.0 0.0 reduce-scatter.7.cloned.1.call-start
  36.0 89.1 %reduce-scatter.5.cloned.1.call-done = bf16[512,2048]{0,1:T(8,128)(2,1)} async-done(((bf16[2048,2048]{0,1:T(8,128)(2,1)}), bf16[512,2048]{0,1:T(8,128)(2,1)}) %reduce-scatter.5.cloned.1.call-update) | async-done | bytes 2097168 | tf_op jit(solution)/shard_map/reduce_scatter | solution.py:359
  125.1 4.0 %copy.17 = bf16[512,2048]{1,0:T(8,128)(2,1)} copy(bf16[512,2048]{0,1:T(8,128)(2,1)} %reduce-scatter.5.cloned.1.call-done) | data formatting | bytes 4194304
  129.1 0.0 reduce-scatter.7.cloned.1.call-update
  129.1 53.8 %shard_map.93 = bf16[2048,2048]{1,0:T(8,128)(2,1)} custom-call(bf16[64,2048]{1,0:T(8,128)(2,1)} %w_ref.1), custom_call_target="tpu_custom_call" | custom-call | tf_op jit(solution)/shard_map/pallas_call | solution.py:338
  182.9 9.0 %convolution_convert_fusion.g_ref = bf16[512,2048]{1,0:T(8,128)(2,1)} fusion(bf16[512,2048]{1,0:T(8,128)(2,1)S(1)} %copy-done, bf16[2048,2048]{1,0:T(8,128)(2,1)} %shard_map.93), kind=kOutput, calls=%fused_computation.1 | convolution fusion | flops 4296015872 | bytes 12582912 | tf_op jit(solution)/shard_map/dot_general | solution.py:366
  191.9 25.2 %shard_map.94 = (bf16[512,2048]{1,0:T(8,128)(2,1)}, bf16[512,2048]{1,0:T(8,128)(2,1)}, bf16[512,2048]{1,0:T(8,128)(2,1)}) custom-call(s32[1,512]{1,0:T(1,128)} %row_ref.3, s32[512,1]{1,0:T(8,128)} %copy.14.col_ref, bf16[512,2048]{1,0:T(8,128)(2,1)} %q_ref.3, bf16[512,2048]{1,0:T(8,128)(2,1)} %k_ref.3, bf16[512,2048]{1,0:T(8,128)(2,1)} %v_ref.3, ...), custom_call_target="tpu_custom_call" | custom-call | flops 5368709120 | bytes 14680064 | tf_op jit(solution)/shard_map/pallas_call | solution.py:102
  217.1 0.0 reduce-scatter.7.cloned.1.call-done
  217.1 2.0 copy.18
  219.1 1.1 convert_multiply_fusion
  220.2 1.1 copy.16
Async XLA Ops:
  7.2 20.4 %copy-start = (bf16[512,2048]{1,0:T(8,128)(2,1)S(1)}, bf16[512,2048]{1,0:T(8,128)(2,1)}, u32[]{:S(2)}) copy-start(bf16[512,2048]{1,0:T(8,128)(2,1)} %param.9) | copy-start | bytes 6291460
  7.2 117.9 %reduce-scatter.5.cloned.1.call-start = ((), (), s32[]{:S(2)}) async-start(), calls=%async_computation.2 | async-start | bytes 10485760 | tf_op jit(solution)/shard_map/reduce_scatter | solution.py:359
  36.0 181.2 %reduce-scatter.7.cloned.1.call-start = ((), (), s32[]{:S(2)}) async-start(), calls=%async_computation.3 | async-start | bytes 2359296
Sparse Core Ops, SparseCore 0:
  36.1 88.9 reduce-scatter.4
  129.2 42.1 reduce-scatter.6

commit v2 on v1

--- a/solution.py
+++ b/solution.py
@@ -328,42 +328,291 @@
     ]
 
 
-def gather_kernel(n_rep, w_ref, all_ref, *sems):
-    for event in gather_events(n_rep, w_ref, all_ref, *sems):
+def interleave(events, work):
+    left = list(work)
+    for at, event in enumerate(events):
         event()
-
-
-def gather_weight(w, n_dp, n_rep):
+        if at < len(events) - 2:
+            if left:
+                left.pop(0)()
+        elif at == len(events) - 2:
+            for piece in left:
+                piece()
+
+
+def loop_work(begin, end, act):
+    def run():
+        lax.fori_loop(begin, end, lambda i, carry: (act(i), carry)[1], 0)
+
+    return run
+
+
+def head_cols(h):
+    return pl.ds(pl.multiple_of(h * DH, DH), DH)
+
+
+def gather_kernel(
+    n_rep, w_ref, row_ref, col_ref, q_ref, k_ref, v_ref, up_ref, all_ref, part_ref,
+    bias, att, *sems,
+):
+    heads = q_ref.shape[1] // DH
+    blocks = up_ref.shape[1] // DH
+
+    def head(h):
+        head_forward(q_ref, k_ref, v_ref, att, bias, head_cols(h))
+
+    def block(i):
+        cols = head_cols(i)
+        part_ref[cols, :] = dot_tn(up_ref[:, cols], att[...]).astype(BF16)
+
+    events = gather_events(n_rep, w_ref, all_ref, *sems)
+    work = [lambda: fill_bias(bias, row_ref, col_ref)]
+    pieces = 6
+    work += [
+        loop_work(heads * i // pieces, heads * (i + 1) // pieces, head) for i in range(pieces)
+    ]
+    pieces = 4
+    work += [
+        loop_work(blocks * i // pieces, blocks * (i + 1) // pieces, block) for i in range(pieces)
+    ]
+    interleave(events, work)
+
+
+def gather_weight(w, ids, qkv, upstream, n_dp, n_rep):
     vm = pl.BlockSpec(memory_space=pltpu.VMEM)
+    size = ids.shape[1]
+    width = qkv[0].shape[1]
     return pl.pallas_call(
         functools.partial(gather_kernel, n_rep),
-        out_shape=jax.ShapeDtypeStruct((n_dp * n_rep * w.shape[0], w.shape[1]), w.dtype),
-        in_specs=[vm],
-        out_specs=vm,
-        scratch_shapes=gather_scratch(n_dp, n_rep),
+        out_shape=[
+            jax.ShapeDtypeStruct((n_dp * n_rep * w.shape[0], width), BF16),
+            jax.ShapeDtypeStruct((upstream.shape[1], width), BF16),
+        ],
+        in_specs=[vm] * 7,
+        out_specs=[vm] * 2,
+        scratch_shapes=[
+            pltpu.VMEM((size, size), F32), pltpu.VMEM((size, width), BF16),
+            *gather_scratch(n_dp, n_rep),
+        ],
         compiler_params=pltpu.CompilerParams(
             collective_id=0, has_side_effects=True, vmem_limit_bytes=VMEM_LIMIT
         ),
-    )(w)
+    )(w, ids, ids.reshape(size, 1), *qkv, upstream)
+
+
+def scatter_events(
+    n_dp, n_rep, scale, part_ref, out_ref, acc, got0, got1, got2, gotz,
+    s0, r0, s1, r1, s2, r2, sz, rz,
+):
+    me = Place(n_rep)
+    depth = out_ref.shape[0]
+    half = depth // 2
+    line = me.line
+    order = ((1, 2), (2, 1))
+    far = 3 - me.dp
+
+    def prows(dp, s, c):
+        return pl.ds(pl.multiple_of(me.shard(dp, s, c) * depth, depth), depth)
+
+    def piece_rows(piece):
+        return pl.ds(piece * half, half)
+
+    def c0(dp, s):
+        return rcopy(
+            part_ref.at[prows(dp, s, 1 - me.c)], got0.at[dp, s], s0.at[dp, s], r0.at[dp, s],
+            me.dev(me.dp, me.r, 1 - me.c),
+        )
+
+    def c1(s, piece, slot):
+        near = me.across(order[piece][0])
+        src = (near, far)[slot]
+        return rcopy(
+            acc.at[src, s, piece_rows(piece)], got1.at[s, piece, slot],
+            s1.at[s, piece, slot], r1.at[s, piece, slot], me.dev(near, me.r, me.c),
+        )
+
+    def c2(s, piece):
+        near = me.across(order[piece][1])
+        return rcopy(
+            acc.at[near, s, piece_rows(piece)], got2.at[s, piece],
+            s2.at[s, piece], r2.at[s, piece], me.dev(near, me.r, me.c),
+        )
+
+    def cz(s, side, to):
+        return rcopy(
+            acc.at[me.dp, s], gotz.at[s, side], sz.at[s], rz.at[s, side], me.dev(me.dp, to, me.c)
+        )
+
+    def zwait(s, side):
+        rcopy(
+            acc.at[me.dp, s], gotz.at[s, side], sz.at[s], rz.at[s, side],
+            me.dev(me.dp, me.r, 1 - me.c),
+        ).wait_recv()
+
+    def each(d, act):
+        if d == 0:
+            act(me.r, None)
+            return
+
+        @pl.when(me.r + d < line)
+        def _():
+            act(me.r + d, 0)
+
+        @pl.when(me.r >= d)
+        def _():
+            act(me.r - d, 1)
+
+    def first():
+        me.greet()
+        for d in reversed(range(line)):
+            each(d, lambda s, side: [c0(dp, s).start() for dp in range(n_dp)] and None)
+
+    def prep(s, side):
+        for dp in range(n_dp):
+            c0(dp, s).wait_recv()
+            acc[dp, s] = (
+                part_ref[prows(dp, s, me.c), :].astype(F32) + got0[dp, s].astype(F32)
+            ).astype(BF16)
+        for slot in (1, 0):
+            for piece in range(2):
+                c1(s, piece, slot).start()
+
+    def mid(s, side):
+        for piece in range(2):
+            near = me.across(order[piece][1])
+            for slot, dp in ((1, near), (0, me.dp)):
+                c1(s, piece, slot).wait_recv()
+                acc[dp, s, piece_rows(piece)] = (
+                    acc[dp, s, piece_rows(piece)].astype(F32) + got1[s, piece, slot].astype(F32)
+                ).astype(BF16)
+                if slot == 1:
+                    c2(s, piece).start()
+
+    def fin(s, side):
+        for piece in range(2):
+            c2(s, piece).wait_recv()
+            acc[me.dp, s, piece_rows(piece)] = (
+                acc[me.dp, s, piece_rows(piece)].astype(F32) + got2[s, piece].astype(F32)
+            ).astype(BF16)
+
+        def add(at):
+            acc[me.dp, s] = (acc[me.dp, s].astype(F32) + gotz[s, at].astype(F32)).astype(BF16)
+
+        def from_below():
+            @pl.when(me.r > 0)
+            def _():
+                zwait(s, 0)
+                if side is None:
+                    out_ref[...] += gotz[s, 0].astype(F32)
+                else:
+                    add(0)
+
+        def from_above():
+            @pl.when(me.r < line - 1)
+            def _():
+                zwait(s, 1)
+                if side is None:
+                    out_ref[...] += gotz[s, 1].astype(F32)
+                else:
+                    add(1)
+
+        if side is None:
+            out_ref[...] = acc[me.dp, s].astype(F32)
+            from_below()
+            from_above()
+            out_ref[...] *= scale
+        elif side == 0:
+            from_below()
+            cz(s, 0, me.r + 1).start()
+        else:
+            from_above()
+            cz(s, 1, me.r - 1).start()
+
+    def drain(s, side):
+        for dp in range(n_dp):
+            c0(dp, s).wait_send()
+        for piece in range(2):
+            for slot in range(2):
+                c1(s, piece, slot).wait_send()
+            c2(s, piece).wait_send()
+        if side == 0:
+            cz(s, 0, me.r + 1).wait_send()
+        elif side == 1:
+            cz(s, 1, me.r - 1).wait_send()
+
+    def event(d, act):
+        return lambda: each(d, act)
+
+    events = [first]
+    dists = list(reversed(range(line)))
+    for at in range(line + 2):
+        if at < line:
+            events.append(event(dists[at], prep))
+        if 0 <= at - 1 < line:
+            events.append(event(dists[at - 1], mid))
+        if 0 <= at - 2 < line:
+            events.append(event(dists[at - 2], fin))
+
+    def finish():
+        for d in dists:
+            each(d, drain)
+
+    events.append(finish)
+    return events
+
+
+def scatter_scratch(n_dp, n_rep, depth, width):
+    line = n_rep // 2
+    half = depth // 2
+    dma = pltpu.SemaphoreType.DMA
+    return [
+        pltpu.VMEM((n_dp, line, depth, width), BF16),
+        pltpu.VMEM((n_dp, line, depth, width), BF16),
+        pltpu.VMEM((line, 2, 2, half, width), BF16),
+        pltpu.VMEM((line, 2, half, width), BF16),
+        pltpu.VMEM((line, 2, depth, width), BF16),
+        dma((n_dp, line)), dma((n_dp, line)),
+        dma((line, 2, 2)), dma((line, 2, 2)),
+        dma((line, 2)), dma((line, 2)),
+        dma((line,)), dma((line, 2)),
+    ]
+
+
+def scatter_kernel(n_dp, n_rep, scale, part_ref, out_ref, *scratch):
+    for event in scatter_events(n_dp, n_rep, scale, part_ref, out_ref, *scratch):
+        event()
+
+
+def scatter_grad(part, scale, n_dp, n_rep):
+    vm = pl.BlockSpec(memory_space=pltpu.VMEM)
+    depth = part.shape[0] // (n_dp * n_rep)
+    return pl.pallas_call(
+        functools.partial(scatter_kernel, n_dp, n_rep, scale),
+        out_shape=jax.ShapeDtypeStruct((depth, part.shape[1]), F32),
+        in_specs=[vm],
+        out_specs=vm,
+        scratch_shapes=scatter_scratch(n_dp, n_rep, depth, part.shape[1]),
+        compiler_params=pltpu.CompilerParams(
+            collective_id=1, has_side_effects=True, vmem_limit_bytes=VMEM_LIMIT
+        ),
+    )(part)
 
 
 def shards(queries, key_rows, values, upstream, out_weight, sample_ids):
     n_dp, n_rep = lax.axis_size("dp"), lax.axis_size("rep")
-    total_tokens = queries.shape[0] * n_dp * n_rep
-    square = n_dp == 4 and n_rep % 2 == 0
+    scale = 1.0 / math.sqrt(queries.shape[0] * n_dp * n_rep)
     qkv = (queries, key_rows, values)
-    (attended,) = attention_call(forward_kernel, sample_ids, qkv, 1, 2)
-    part = lax.dot_general(
-        upstream, attended, (((0,), (0,)), ((), ())), preferred_element_type=F32
-    ).astype(BF16)
-    group_sums = lax.psum_scatter(part, "dp", scatter_dimension=0, tiled=True)
-    summed = lax.psum_scatter(group_sums, "rep", scatter_dimension=0, tiled=True)
-    grad_weight = summed.astype(F32) * (1.0 / math.sqrt(total_tokens))
-    if square:
-        weight = gather_weight(out_weight, n_dp, n_rep)
+    if n_dp == 4 and n_rep % 2 == 0:
+        weight, part = gather_weight(out_weight, sample_ids, qkv, upstream, n_dp, n_rep)
+        grad_weight = scatter_grad(part, scale, n_dp, n_rep)
     else:
+        (attended,) = attention_call(forward_kernel, sample_ids, qkv, 1, 2)
+        part = dot_tn(upstream, attended).astype(BF16)
+        group_sums = lax.psum_scatter(part, "dp", scatter_dimension=0, tiled=True)
+        summed = lax.psum_scatter(group_sums, "rep", scatter_dimension=0, tiled=True)
+        grad_weight = summed.astype(F32) * scale
         weight = lax.all_gather(out_weight, ("dp", "rep"), axis=0, tiled=True)
-    grad_attended = jnp.dot(upstream, weight, preferred_element_type=F32).astype(BF16)
+    grad_attended = dot_nn(upstream, weight).astype(BF16)
     grads = attention_call(backward_kernel, sample_ids, qkv + (grad_attended,), 3, 5)
     return (*grads, grad_weight)
 

time: 229 us -> 141 us (0.62)
  waiting for transfers between devices: 89.1 us -> 0 us
  Pallas kernels: 97.6 us -> 128 us
  between operations: 14.1 us -> 0.67 us
  matrix products: 17.4 us -> 9.09 us
  local copies, waits for them, and re-layouts: 8.71 us -> 2.34 us
    reduce_scatter x1 -> x0, waiting for transfers between devices: 89.1 us -> none  [shards(): group_sums = lax.psum_scatter(part, 'dp', scatter_dimension=0, tiled=True)]
    pallas_call x1 -> x2, Pallas kernels: 53.8 us -> 103 us  [the longest x1 52.5 us: gather_weight(): pl.pallas_call(functools.partial(gather_kernel, n_rep), out_shape=[jax.Sh...]
    pallas_call x2 -> x1, Pallas kernels: 43.8 us -> 25.3 us  [attention_call(): pl.pallas_call(kernel, grid=(heads,), out_shape=[jax.ShapeDtypeStruct(arr...]
    dot_general x2 -> x1, matrix products: 17.4 us -> 9.09 us  [dot_nn(): return jnp.dot(a, b, preferred_element_type=F32)]
    unnamed x5, local copies, waits for them, and re-layouts: 7.03 us -> 0.8 us
  transfers between devices with their start and end apart: 2 -> 0, of which waited for: 1 -> 0; matrix products, arithmetic and copies ran while one was open for 4% -> 0% of each run, Pallas kernels for 35% -> 0%
where the time goes in v2:
time: 141 us; the launch traced here: 140 us
  Pallas kernels  128 us (91%)
  matrix products  9.09 us (6%)
  local copies, waits for them, and re-layouts  2.34 us (2%)
    pallas_call x1, Pallas kernels, gather_weight(): pl.pallas_call(functools.partial(gather_kernel, n_rep), out_shape=[jax.Sh...  52.5 us
    pallas_call x1, Pallas kernels, scatter_grad(): pl.pallas_call(functools.partial(scatter_kernel, n_dp, n_rep, scale), out...  50.2 us
    pallas_call x1, Pallas kernels, attention_call(): pl.pallas_call(kernel, grid=(heads,), out_shape=[jax.ShapeDtypeStruct(arr...  25.3 us
    dot_general x1, matrix products, dot_nn(): return jnp.dot(a, b, preferred_element_type=F32)  9.09 us

profile of v2, /device:TPU:0, one launch (start us, length us, event | category | flops | bytes accessed | tf_op | source)
XLA Modules:
  0.0 140.1 jit_solution(2731095113088026040)
XLA Ops:
  0.6 1.5 %copy.13.col_ref = s32[512,1]{1,0:T(8,128)} copy(s32[512,1]{0,1:T(1,128)} %bitcast.5) | data formatting | bytes 4096 | tf_op jit(solution)/shard_map/reshape | solution.py:115
  2.2 0.0 copy-start
  2.2 52.5 %shard_map.93 = (bf16[2048,2048]{1,0:T(8,128)(2,1)}, bf16[2048,2048]{1,0:T(8,128)(2,1)}) custom-call(bf16[64,2048]{1,0:T(8,128)(2,1)} %w_ref.1, s32[1,512]{1,0:T(1,128)} %row_ref.3, s32[512,1]{1,0:T(8,128)} %copy.13.col_ref, bf16[512,2048]{1,0:T(8,128)(2,1)} %q_ref.3, bf16[512,2048]{1,0:T(8,128)(2,1)} %k_ref.3, bf16[512,2048]{1,0:T(8,128)(2,1)} %v_ref.3, ...), custom_call_target="tpu_custom_call" | custom-call | tf_op jit(solution)/shard_map/pallas_call | solution.py:385
  54.7 0.0 copy-done
  54.7 9.1 %fusion.g_ref = bf16[512,2048]{1,0:T(8,128)(2,1)} fusion(bf16[512,2048]{1,0:T(8,128)(2,1)S(1)} %copy-done, bf16[2048,2048]{1,0:T(8,128)(2,1)} %get-tuple-element.9), kind=kOutput, calls=%fused_computation.1 | convolution fusion | flops 4296015872 | bytes 12582912 | tf_op jit(solution)/shard_map/dot_general | solution.py:28
  63.8 50.2 %shard_map.95 = f32[64,2048]{1,0:T(8,128)} custom-call(bf16[2048,2048]{1,0:T(8,128)(2,1)} %get-tuple-element.13.part_ref), custom_call_target="tpu_custom_call" | custom-call | tf_op jit(solution)/shard_map/pallas_call | solution.py:589
  114.0 0.0 copy-start.1
  114.0 25.3 %shard_map.94 = (bf16[512,2048]{1,0:T(8,128)(2,1)}, bf16[512,2048]{1,0:T(8,128)(2,1)}, bf16[512,2048]{1,0:T(8,128)(2,1)}) custom-call(s32[1,512]{1,0:T(1,128)} %row_ref.3, s32[512,1]{1,0:T(8,128)} %copy.13.col_ref, bf16[512,2048]{1,0:T(8,128)(2,1)} %q_ref.3, bf16[512,2048]{1,0:T(8,128)(2,1)} %k_ref.3, bf16[512,2048]{1,0:T(8,128)(2,1)} %v_ref.3, ...), custom_call_target="tpu_custom_call" | custom-call | flops 5368709120 | bytes 14680064 | tf_op jit(solution)/shard_map/pallas_call | solution.py:102
  139.3 0.0 copy-done.1
  139.3 0.8 copy.16
Async XLA Ops:
  2.2 52.6 %copy-start = (bf16[512,2048]{1,0:T(8,128)(2,1)S(1)}, bf16[512,2048]{1,0:T(8,128)(2,1)}, u32[]{:S(2)}) copy-start(bf16[512,2048]{1,0:T(8,128)(2,1)} %up_ref.1) | copy-start | bytes 6291460
  114.0 25.3 %copy-start.1 = (f32[64,2048]{1,0:T(8,128)S(1)}, f32[64,2048]{1,0:T(8,128)}, u32[]{:S(2)}) copy-start(f32[64,2048]{1,0:T(8,128)} %shard_map.95) | copy-start | bytes 1572868
